TPU v7x, 32 devices: a whole 2x2x4 slice. The times are simulated.
32 devices in a mesh: grp: 2 (over x), blk: 16 (over z, y, core).
Axes of the slice: x: 2, y: 2, z: 4, core: 2. Of those that a mesh axis runs over, the one named last changes fastest.
Arguments:
- sensors: float32 [3, 32768], P(None, 'blk'), may hold values from 0 to 1
- sources: bfloat16 [3, 65536], P(None, ('grp', 'blk')), may hold values from 0 to 1
- weights: bfloat16 [65536], P(('grp', 'blk')), may hold values from 0.5 to 2
- probes: bfloat16 [65536, 128], P(('grp', 'blk')), may hold values from -6 to 6
Outputs:
- response: float32 [128, 32768], P('grp', 'blk')
All inputs are finite; a program needn't handle non-finite values.
Results may differ from a plain program's by a relative error of at most 0.01.
Values may be sent and summed in bfloat16 or wider, within the bound.
A program may use at most 64 MiB of HBM per device.

v0:
```python
import functools
import math

import jax
import jax.numpy as jnp
from jax import lax
from jax.experimental import pallas as pl
from jax.experimental.pallas import tpu as pltpu
from jax.sharding import PartitionSpec as P

STEPS = 6
SLOTS = STEPS + 1
EPS = 0.0025
FEAT = 16
CHUNKS = 4
QUARTERS = 4
TILE = 256
MESH = pl.DeviceIdType.MESH


def pieces(x):
    hi = x.astype(jnp.bfloat16)
    rest = x - hi.astype(jnp.float32)
    mid = rest.astype(jnp.bfloat16)
    lo = (rest - mid.astype(jnp.float32)).astype(jnp.bfloat16)
    return [hi.astype(jnp.float32), mid.astype(jnp.float32), lo.astype(jnp.float32)]


def body(groups, n_blk, scale, sens_ref, src_ref, wgt_ref, prb_ref, out_ref,
         bufs, feat, acc, part, got, send_sem, recv_sem, psend_sem, precv_sem):
    chunk = bufs.shape[3]
    probes = prb_ref.shape[1]
    sensors = sens_ref.shape[1]
    rows = probes // groups
    quarter = sensors // QUARTERS
    chips = n_blk // 2

    grp = lax.axis_index("grp")
    me = lax.axis_index("blk")
    chip = me // 2
    core = me % 2
    odd = chip % 2
    ahead = 2 * ((chip + 2) % chips) + core
    behind = 2 * ((chip + chips - 2) % chips) + core
    peer = 2 * (chip + 1 - 2 * odd) + core
    twin = 2 * chip + 1 - core

    barrier = pltpu.get_barrier_semaphore()
    for other in (ahead, behind, peer, twin):
        pl.semaphore_signal(barrier, inc=1, device_id=(grp, other), device_id_type=MESH)
    for k in range(1, groups):
        pl.semaphore_signal(barrier, inc=1, device_id=((grp + k) % groups, me), device_id_type=MESH)

    for j in range(CHUNKS):
        cols = pl.ds(j * chunk, chunk)
        turned = jnp.transpose(prb_ref[cols, :].astype(jnp.float32))
        bufs[0, j, :probes, :] = (turned * wgt_ref[:, cols].astype(jnp.float32)).astype(jnp.bfloat16)
        s = src_ref[:, cols].astype(jnp.float32)
        square = jnp.sum(s * s, axis=0, keepdims=True)
        one = jnp.ones((1, chunk), jnp.float32)
        bufs[0, j, probes:, :] = jnp.concatenate(
            [s, s, s] + pieces(square) + [one, one, one, 0.0 * one], axis=0
        ).astype(jnp.bfloat16)
    x = sens_ref[...]
    square = jnp.sum(x * x, axis=0, keepdims=True) + EPS
    one = jnp.ones((1, sensors), jnp.float32)
    feat[...] = jnp.concatenate(
        [-2.0 * p for p in pieces(x)] + [one, one, one] + pieces(square) + [0.0 * one], axis=0
    ).astype(jnp.bfloat16)

    def copy(kind, src_slot, dst_slot, j, other):
        return pltpu.make_async_remote_copy(
            src_ref=bufs.at[src_slot, j],
            dst_ref=bufs.at[dst_slot, j],
            send_sem=send_sem.at[kind, j],
            recv_sem=recv_sem.at[dst_slot, j],
            device_id=(grp, other),
            device_id_type=MESH,
        )

    def arrived(slot, j):
        copy(0, slot, slot, j, ahead).wait_recv()

    def far(j): return copy(0, 0, 4, j, ahead)
    def near(j): return copy(1, 4 * odd, 2, j, peer)
    def relay_far(j): return copy(2, 2, 6, j, ahead)
    def relay_near(j): return copy(3, 4, 6, j, peer)
    def twin_own(j): return copy(4, 0, 1, j, twin)
    def twin_four(j): return copy(5, 4, 5 - 2 * core, j, twin)
    def twin_two(j): return copy(6, 2, 3 - 2 * core, j, twin)
    def twin_six(j): return copy(7, 6, 5, j, twin)

    relays = jnp.logical_and(odd == 0, core == 1)

    pl.semaphore_wait(barrier, 4 + groups - 1)
    for j in range(CHUNKS):
        far(j).start()

        @pl.when(odd == 0)
        def _():
            near(j).start()

        @pl.when(core == 0)
        def _():
            twin_own(j).start()

    acc[...] = jnp.zeros_like(acc)

    def span(slot, j, start, width):
        f = bufs[slot, j, probes:, :]
        p = bufs[slot, j, :probes, :]
        for t in range(width // TILE):
            cols = pl.ds(start + t * TILE, TILE)
            dist = lax.dot_general(f, feat[:, cols], (((0,), (0,)), ((), ())),
                                   preferred_element_type=jnp.float32)
            ker = lax.rsqrt(dist.astype(jnp.bfloat16))
            acc[:, cols] += jnp.dot(p, ker, preferred_element_type=jnp.float32)

    def unit(slot, j):
        span(slot, j, 0, sensors)

    def own(j, _):
        unit(0, j)
        return 0

    lax.fori_loop(0, CHUNKS, own, 0)

    def middle(j, _):
        @pl.when(j < CHUNKS)
        def _():
            arrived(4, j)
            twin_four(j).start()

            @pl.when(odd == 1)
            def _():
                near(j).start()

            @pl.when(relays)
            def _():
                relay_near(j).start()

        @pl.when(j >= 1)
        def _():
            arrived(2, j - 1)
            twin_two(j - 1).start()

            @pl.when(relays)
            def _():
                relay_far(j - 1).start()

            unit(2, j - 1)
            arrived(1 + 2 * core, j - 1)
            unit(1 + 2 * core, j - 1)

        @pl.when(j < CHUNKS)
        def _():
            unit(4, j)
            arrived(3 + 2 * core, j)
            unit(3 + 2 * core, j)
        return 0

    lax.fori_loop(0, CHUNKS + 1, middle, 0)

    last = 5 - 4 * core

    def fetch(j):
        @pl.when(core == 1)
        def _():
            arrived(6, j)
            twin_six(j).start()
        arrived(last, j)

    def final(j, _):
        fetch(j)
        unit(last, j)
        return 0

    lax.fori_loop(0, CHUNKS - 1, final, 0)
    fetch(CHUNKS - 1)

    def swap(q, k):
        return pltpu.make_async_remote_copy(
            src_ref=part.at[q, k - 1],
            dst_ref=got.at[q, k - 1],
            send_sem=psend_sem.at[q, k - 1],
            recv_sem=precv_sem.at[q, k - 1],
            device_id=((grp + k) % groups, me),
            device_id_type=MESH,
        )

    for q in range(QUARTERS):
        cols = pl.ds(q * quarter, quarter)
        span(last, CHUNKS - 1, q * quarter, quarter)
        for k in range(1, groups):
            take = pl.ds(pl.multiple_of(((grp + k) % groups) * rows, 8), rows)
            part[q, k - 1] = (acc[take, cols] * scale).astype(jnp.bfloat16)
            swap(q, k).start()
    for q in range(QUARTERS):
        cols = pl.ds(q * quarter, quarter)
        total = acc[pl.ds(pl.multiple_of(grp * rows, 8), rows), cols] * scale
        for k in range(1, groups):
            swap(q, k).wait_recv()
            total = total + got[q, k - 1].astype(jnp.float32)
        out_ref[:, cols] = total
        for k in range(1, groups):
            swap(q, k).wait_send()

    for j in range(CHUNKS):
        far(j).wait_send()
        near(j).wait_send()
        twin_four(j).wait_send()
        twin_two(j).wait_send()

        @pl.when(relays)
        def _():
            relay_far(j).wait_send()
            relay_near(j).wait_send()

        @pl.when(core == 0)
        def _():
            twin_own(j).wait_send()

        @pl.when(core == 1)
        def _():
            twin_six(j).wait_send()


def shards(sensors, sources, weights, probes):
    groups = lax.axis_size("grp")
    n_blk = lax.axis_size("blk")
    n_src, n_probe = probes.shape
    n_sens = sensors.shape[1]
    chunk = n_src // CHUNKS
    rows = n_probe // groups
    quarter = n_sens // QUARTERS
    scale = 1.0 / math.sqrt(STEPS * n_src * groups)
    vmem = pl.BlockSpec(memory_space=pltpu.VMEM)
    return pl.pallas_call(
        functools.partial(body, groups, n_blk, scale),
        out_shape=jax.ShapeDtypeStruct((rows, n_sens), jnp.float32),
        in_specs=[vmem] * 4,
        out_specs=vmem,
        scratch_shapes=[
            pltpu.VMEM((SLOTS, CHUNKS, n_probe + FEAT, chunk), jnp.bfloat16),
            pltpu.VMEM((FEAT, n_sens), jnp.bfloat16),
            pltpu.VMEM((n_probe, n_sens), jnp.float32),
            pltpu.VMEM((QUARTERS, groups - 1, rows, quarter), jnp.bfloat16),
            pltpu.VMEM((QUARTERS, groups - 1, rows, quarter), jnp.bfloat16),
            pltpu.SemaphoreType.DMA((8, CHUNKS)),
            pltpu.SemaphoreType.DMA((SLOTS, CHUNKS)),
            pltpu.SemaphoreType.DMA((QUARTERS, groups - 1)),
            pltpu.SemaphoreType.DMA((QUARTERS, groups - 1)),
        ],
        compiler_params=pltpu.CompilerParams(collective_id=0, has_side_effects=True),
    )(sensors, sources, weights.reshape(1, n_src), probes)


def solution(mesh):
    in_specs = (P(None, "blk"), P(None, ("grp", "blk")), P(("grp", "blk")), P(("grp", "blk"), None))
    out_specs = P("grp", "blk")
    return jax.shard_map(shards, mesh=mesh, in_specs=in_specs, out_specs=out_specs, check_vma=False)
```

profile of v0, /device:TPU:0, one launch (start us, length us, event | category | flops | bytes accessed | tf_op | source)
XLA Modules:
  0.0 76.8 jit_solution(10984525244848908398)
XLA Ops:
  0.0 1.3 %reshape.3.wgt_ref = bf16[1,2048]{1,0:T(2,128)(2,1)} reshape(bf16[2048]{0:T(1024)(128)(2,1)} %param.6) | data formatting | bytes 8192 | tf_op jit(solution)/shard_map/reshape | solution.py:255
  1.3 73.6 %shard_map.46 = f32[64,2048]{1,0:T(8,128)} custom-call(f32[3,2048]{1,0:T(4,128)} %sens_ref.1, bf16[3,2048]{1,0:T(4,128)(2,1)} %src_ref.1, bf16[1,2048]{1,0:T(2,128)(2,1)} %reshape.3.wgt_ref, bf16[2048,128]{1,0:T(8,128)(2,1)} %prb_ref.1), custom_call_target="tpu_custom_call" | custom-call | tf_op jit(solution)/shard_map/pallas_call | solution.py:238
  74.9 1.9 %copy.6 = f32[64,2048]{1,0:T(8,128)} copy(f32[64,2048]{1,0:T(8,128)} %shard_map.46) | data formatting | bytes 1048576
where the time goes:
time: 77 us; the launch traced here: 76.8 us
  Pallas kernels  73.6 us (96%)
  local copies, waits for them, and re-layouts  3.16 us (4%)
    pallas_call x1, Pallas kernels, shards(): pl.pallas_call(functools.partial(body, groups, n_blk, scale), out_shape=j...  73.6 us
    unnamed x1, local copies, waits for them, and re-layouts  1.87 us

commit v1 on v0

--- a/solution.py
+++ b/solution.py
@@ -14,7 +14,7 @@
 FEAT = 16
 CHUNKS = 4
 QUARTERS = 4
-TILE = 256
+TILE = 1024
 MESH = pl.DeviceIdType.MESH
 
 
@@ -54,7 +54,7 @@
     for j in range(CHUNKS):
         cols = pl.ds(j * chunk, chunk)
         turned = jnp.transpose(prb_ref[cols, :].astype(jnp.float32))
-        bufs[0, j, :probes, :] = (turned * wgt_ref[:, cols].astype(jnp.float32)).astype(jnp.bfloat16)
+        bufs[0, j, :probes, :] = (turned * wgt_ref[cols].astype(jnp.float32)[None, :]).astype(jnp.bfloat16)
         s = src_ref[:, cols].astype(jnp.float32)
         square = jnp.sum(s * s, axis=0, keepdims=True)
         one = jnp.ones((1, chunk), jnp.float32)
@@ -109,8 +109,9 @@
     def span(slot, j, start, width):
         f = bufs[slot, j, probes:, :]
         p = bufs[slot, j, :probes, :]
-        for t in range(width // TILE):
-            cols = pl.ds(start + t * TILE, TILE)
+        tile = min(TILE, width)
+        for t in range(width // tile):
+            cols = pl.ds(start + t * tile, tile)
             dist = lax.dot_general(f, feat[:, cols], (((0,), (0,)), ((), ())),
                                    preferred_element_type=jnp.float32)
             ker = lax.rsqrt(dist.astype(jnp.bfloat16))
@@ -125,32 +126,48 @@
 
     lax.fori_loop(0, CHUNKS, own, 0)
 
+    def got_four(j):
+        arrived(4, j)
+        twin_four(j).start()
+
+        @pl.when(odd == 1)
+        def _():
+            near(j).start()
+
+        @pl.when(relays)
+        def _():
+            relay_near(j).start()
+
+    def got_two(j):
+        arrived(2, j)
+        twin_two(j).start()
+
+        @pl.when(relays)
+        def _():
+            relay_far(j).start()
+
     def middle(j, _):
-        @pl.when(j < CHUNKS)
-        def _():
-            arrived(4, j)
-            twin_four(j).start()
-
-            @pl.when(odd == 1)
-            def _():
-                near(j).start()
-
-            @pl.when(relays)
-            def _():
-                relay_near(j).start()
+        @pl.when(j <= 1)
+        def _():
+            got_four(j)
+
+        @pl.when(jnp.logical_and(j >= 1, j <= 2))
+        def _():
+            got_two(j - 1)
 
         @pl.when(j >= 1)
         def _():
-            arrived(2, j - 1)
-            twin_two(j - 1).start()
-
-            @pl.when(relays)
-            def _():
-                relay_far(j - 1).start()
-
             unit(2, j - 1)
             arrived(1 + 2 * core, j - 1)
             unit(1 + 2 * core, j - 1)
+
+        @pl.when(jnp.logical_and(j >= 1, j + 1 < CHUNKS))
+        def _():
+            got_four(j + 1)
+
+        @pl.when(jnp.logical_and(j >= 2, j < CHUNKS))
+        def _():
+            got_two(j)
 
         @pl.when(j < CHUNKS)
         def _():
@@ -163,20 +180,13 @@
 
     last = 5 - 4 * core
 
-    def fetch(j):
-        @pl.when(core == 1)
-        def _():
+    @pl.when(core == 1)
+    def _():
+        for j in range(CHUNKS):
             arrived(6, j)
             twin_six(j).start()
+    for j in range(CHUNKS):
         arrived(last, j)
-
-    def final(j, _):
-        fetch(j)
-        unit(last, j)
-        return 0
-
-    lax.fori_loop(0, CHUNKS - 1, final, 0)
-    fetch(CHUNKS - 1)
 
     def swap(q, k):
         return pltpu.make_async_remote_copy(
@@ -190,7 +200,8 @@
 
     for q in range(QUARTERS):
         cols = pl.ds(q * quarter, quarter)
-        span(last, CHUNKS - 1, q * quarter, quarter)
+        for j in range(CHUNKS):
+            span(last, j, q * quarter, quarter)
         for k in range(1, groups):
             take = pl.ds(pl.multiple_of(((grp + k) % groups) * rows, 8), rows)
             part[q, k - 1] = (acc[take, cols] * scale).astype(jnp.bfloat16)
@@ -252,7 +263,7 @@
             pltpu.SemaphoreType.DMA((QUARTERS, groups - 1)),
         ],
         compiler_params=pltpu.CompilerParams(collective_id=0, has_side_effects=True),
-    )(sensors, sources, weights.reshape(1, n_src), probes)
+    )(sensors, sources, weights, probes)
 
 
 def solution(mesh):

time: 77 us -> 48.4 us (0.63)
  Pallas kernels: 73.6 us -> 46.3 us
  local copies, waits for them, and re-layouts: 3.16 us -> 1.87 us
    pallas_call x1, Pallas kernels: 73.6 us -> 46.3 us  [shards(): pl.pallas_call(functools.partial(body, groups, n_blk, scale), out_shape=j...]
    reshape x1 -> x0, local copies, waits for them, and re-layouts: 1.29 us -> none  [shards(): weights.reshape(1, n_src)]
where the time goes in v1:
time: 48.4 us; the launch traced here: 48.2 us
  Pallas kernels  46.3 us (96%)
  local copies, waits for them, and re-layouts  1.87 us (4%)
    pallas_call x1, Pallas kernels, shards(): pl.pallas_call(functools.partial(body, groups, n_blk, scale), out_shape=j...  46.3 us
    unnamed x1, local copies, waits for them, and re-layouts  1.87 us

profile of v1, /device:TPU:0, one launch (start us, length us, event | category | flops | bytes accessed | tf_op | source)
XLA Modules:
  0.0 48.2 jit_solution(11236922230393998976)
XLA Ops:
  0.0 46.3 %shard_map.46 = f32[64,2048]{1,0:T(8,128)} custom-call(f32[3,2048]{1,0:T(4,128)} %sens_ref.1, bf16[3,2048]{1,0:T(4,128)(2,1)} %src_ref.1, bf16[2048]{0:T(1024)(128)(2,1)} %wgt_ref.1, bf16[2048,128]{1,0:T(8,128)(2,1)} %prb_ref.1), custom_call_target="tpu_custom_call" | custom-call | tf_op jit(solution)/shard_map/pallas_call | solution.py:249
  46.3 1.9 %copy.6 = f32[64,2048]{1,0:T(8,128)} copy(f32[64,2048]{1,0:T(8,128)} %shard_map.46) | data formatting | bytes 1048576
